TPU v7x, 512 devices: a whole 4x8x8 slice. The times are simulated.
512 devices in a mesh: seq: 16 (over z, core), exp: 32 (over y, x).
Axes of the slice: x: 4, y: 8, z: 8, core: 2. Of those that a mesh axis runs over, the one named last changes fastest.
Arguments:
- residual_in: bfloat16 [1024, 32, 1152], P('seq', 'exp'), may hold values from -6 to 6
- query_proj: bfloat16 [1024, 32, 1152], P('seq', 'exp'), may hold values from -6 to 6
- key_proj: bfloat16 [1024, 32, 1152], P('seq', 'exp'), may hold values from -6 to 6
- value_proj: bfloat16 [1024, 32, 1152], P('seq', 'exp'), may hold values from -6 to 6
- out_weight: bfloat16 [1152, 1152], replicated, may hold values from -0.1875 to 0.1875
- router_weight: bfloat16 [1152, 16], replicated, may hold values from -0.1875 to 0.1875
- first_weight: bfloat16 [32, 1152, 2304], P('exp', None, 'seq'), may hold values from -0.1875 to 0.1875
- second_weight: bfloat16 [32, 2304, 1152], P('exp', 'seq'), may hold values from -0.09375 to 0.09375
- class_table: bfloat16 [1024, 4, 1152], P('seq'), may hold values from -3 to 3
- time_weight: bfloat16 [256, 4, 1152], P('seq'), may hold values from -0.375 to 0.375
- class_labels: int32 [32], P('exp'), may hold values from 0 to 1023
- timesteps: int32 [32], P('exp'), may hold values from 0 to 999
- expert_ids: int32 [16, 32, 64, 1, 2], P('seq', 'exp'), may hold values from 0 to 15, all different within a row; in each aligned block of 64 rows (0 to 63, 64 to 127, ..., all dimensions but the last counted through in order) at most 10 rows name the same one
Outputs:
- block_out: bfloat16 [1024, 32, 1152], P('seq', 'exp')
Inputs may be any that keep to these rules, and one draw needn't show every extreme that they name: `expert_ids`: each row names 2 different experts; among the rows of one device no expert is named by more than 10 rows.
All inputs are finite; a program needn't handle non-finite values.
Results may differ from a plain program's by a relative error of at most 0.013.
Values may be sent and summed in bfloat16 or wider, within the bound.
A program may use at most 64 MiB of HBM per device.

v0:
```python
import math

import jax
import jax.numpy as jnp
from jax import lax
from jax.sharding import PartitionSpec as P

HEAD = 72
FREQ = 256


def turned_gather(arrays, axis, dims):
    turned = [jnp.moveaxis(a, dim, 0) for a, dim in zip(arrays, dims)]
    both = jnp.concatenate([t.reshape(len(t), -1) for t in turned], axis=1)
    out, at, finished = (lax.all_gather(both, axis, axis=0, tiled=True), 0, [])
    for t, dim in zip(turned, dims):
        share = out[:, at : at + t[0].size].reshape(-1, *t.shape[1:])
        finished.append(jnp.moveaxis(share, 0, dim))
        at += t[0].size
    return tuple(finished)


def from_everyone(value, axis):
    peers = lax.axis_size(axis)
    return lax.all_to_all(
        jnp.broadcast_to(value[None], (peers, *value.shape)), axis, 0, 0, tiled=True
    )


def taken_together(value, axis):
    return from_everyone(value, axis).sum(axis=0)


def side_by_side(arrays, axis, split_dim, concat_dim, along):
    both = jnp.concatenate(arrays, axis=along)
    out, at, finished = (
        lax.all_to_all(both, axis, split_axis=split_dim, concat_axis=concat_dim, tiled=True),
        0,
        [],
    )
    for a in arrays:
        finished.append(lax.slice_in_dim(out, at, at + a.shape[along], axis=along))
        at += a.shape[along]
    return tuple(finished)


def swapped(block, axis, stride):
    count = lax.axis_size(axis)
    route = []
    for low in range(count):
        high = low | 1 << stride
        if high != low and high < count:
            route += [(low, high), (high, low)]
    return lax.ppermute(block, axis, route)


def time_embed(timesteps):
    half_width = FREQ // 2
    frequencies = jnp.exp(
        -math.log(10000.0) * jnp.arange(half_width, dtype=jnp.float32) / half_width
    )
    angles = timesteps.astype(jnp.float32)[:, None] * frequencies[None, :]
    return jnp.concatenate([jnp.cos(angles), jnp.sin(angles)], axis=1)


def body(
    residual_in,
    query_proj,
    key_proj,
    value_proj,
    out_weight,
    router_weight,
    first_weight,
    second_weight,
    class_table,
    time_weight,
    class_labels,
    timesteps,
    expert_ids,
):
    seq_dev, img_dev, model_width = residual_in.shape
    heads_here = query_proj.shape[2] // HEAD
    token_count = seq_dev * img_dev
    inv_root = 1.0 / math.sqrt(HEAD)
    full_first, full_second = turned_gather((first_weight[0], second_weight[0]), "seq", (1, 0))
    table_rows = class_table.shape[0]
    seq_place = lax.axis_index("seq")
    lowest = seq_place * table_rows
    picker = (
        class_labels[:, None] - lowest == jnp.arange(table_rows, dtype=jnp.int32)[None, :]
    ).astype(jnp.bfloat16)
    class_part = jnp.dot(
        picker, class_table.reshape(table_rows, -1), preferred_element_type=jnp.float32
    )
    freq_rows = time_weight.shape[0]
    embedded = time_embed(timesteps)
    own_freq = lax.dynamic_slice_in_dim(embedded, seq_place * freq_rows, freq_rows, 1)
    time_part = jnp.dot(
        own_freq,
        time_weight.reshape(freq_rows, -1).astype(jnp.float32),
        precision=lax.Precision.HIGHEST,
    )
    conditions = taken_together(class_part + time_part, "seq").reshape(img_dev, 4, model_width)
    groups = img_dev * heads_here
    query_items = query_proj.reshape(seq_dev, groups, HEAD)
    key_items = key_proj.reshape(seq_dev, groups, HEAD)
    value_items = value_proj.reshape(seq_dev, groups, HEAD)
    query_full, key_full, value_full = side_by_side(
        (query_items, key_items, value_items), "seq", 1, 0, 2
    )
    scores = (
        jnp.einsum("qge,kge->gqk", query_full, key_full, preferred_element_type=jnp.float32)
        * inv_root
    )
    row_max = jnp.max(scores, axis=-1, keepdims=True)
    exp_scores = jnp.exp(scores - row_max)
    row_total = jnp.sum(exp_scores, axis=-1, keepdims=True)
    mixed_out = jnp.einsum(
        "gqk,kge->qge",
        exp_scores.astype(jnp.bfloat16),
        value_full,
        preferred_element_type=jnp.float32,
    )
    mixed_out = (mixed_out / jnp.transpose(row_total, (1, 0, 2))).astype(jnp.bfloat16)
    attended = lax.all_to_all(mixed_out, "seq", split_axis=0, concat_axis=1, tiled=True).reshape(
        seq_dev, img_dev, heads_here * HEAD
    )
    projected = jnp.dot(
        attended.reshape(token_count, -1), out_weight, preferred_element_type=jnp.float32
    ).reshape(seq_dev, img_dev, model_width)
    updated = (residual_in.astype(jnp.float32) + conditions[None, :, 0, :] * projected).astype(
        jnp.bfloat16
    )
    updated_f = updated.astype(jnp.float32)
    mean_value = jnp.mean(updated_f, axis=-1, keepdims=True)
    centered = updated_f - mean_value
    variance = jnp.mean(centered * centered, axis=-1, keepdims=True)
    normed = centered * lax.rsqrt(variance + 1e-06)
    moe_in = (normed * (1.0 + conditions[None, :, 2, :]) + conditions[None, :, 1, :]).astype(
        jnp.bfloat16
    )
    moe_rows = moe_in.reshape(token_count, model_width)
    experts_all = router_weight.shape[1]
    top_count = expert_ids.shape[-1]
    capacity = max(2, 5 * token_count * top_count // (4 * experts_all))
    logits = jnp.dot(moe_rows, router_weight, preferred_element_type=jnp.float32)
    ids_local = expert_ids.reshape(-1)
    onehot = (ids_local[:, None] == jnp.arange(experts_all, dtype=jnp.int32)[None, :]).astype(
        jnp.int32
    )
    chosen = jnp.sum(
        onehot.reshape(token_count, top_count, experts_all).astype(jnp.float32)
        * logits[:, None, :],
        axis=-1,
    )
    first_share = jax.nn.sigmoid(chosen[:, 0] - chosen[:, 1])
    slot_index = jnp.sum(jnp.cumsum(onehot, axis=0) * onehot, axis=1) - 1
    dest_index = ids_local * capacity + slot_index
    source_rows = jnp.repeat(moe_rows, top_count, axis=0)
    outgoing = (
        jnp.zeros((experts_all * capacity, model_width), jnp.bfloat16)
        .at[dest_index]
        .set(source_rows)
    )
    outgoing = jnp.repeat(outgoing.reshape(experts_all, capacity, model_width), 2, axis=0)
    arrived = lax.all_to_all(outgoing, "exp", split_axis=0, concat_axis=0, tiled=True)
    flat_rows = arrived.reshape(-1, model_width)
    pre_act = jnp.dot(flat_rows, full_first, preferred_element_type=jnp.float32)
    inner_act = jax.nn.gelu(pre_act, approximate=True).astype(jnp.bfloat16)
    result = jnp.dot(inner_act, full_second, preferred_element_type=jnp.float32).astype(
        jnp.bfloat16
    )
    partial_out = result.reshape(arrived.shape)
    partner_out = swapped(partial_out, "exp", 0)
    produced = (partial_out.astype(jnp.float32) + partner_out.astype(jnp.float32)).astype(
        jnp.bfloat16
    )
    half_width = model_width // 2
    own_half = lax.axis_index("exp") % 2
    produced_half = lax.dynamic_slice_in_dim(produced, own_half * half_width, half_width, 2)
    returned = lax.all_to_all(produced_half, "exp", split_axis=0, concat_axis=0, tiled=True)
    returned = (
        returned.reshape(experts_all, 2, capacity, half_width)
        .transpose(0, 2, 1, 3)
        .reshape(experts_all * capacity, model_width)
    )
    picked = returned[dest_index].reshape(token_count, top_count, model_width).astype(jnp.float32)
    moe_out = (
        first_share[:, None] * picked[:, 0, :] + (1.0 - first_share)[:, None] * picked[:, 1, :]
    )
    moe_out = moe_out.reshape(seq_dev, img_dev, model_width)
    return (updated_f + conditions[None, :, 3, :] * moe_out).astype(jnp.bfloat16)


def solution(mesh):
    return jax.shard_map(
        body,
        mesh=mesh,
        in_specs=(
            P("seq", "exp", None),
            P("seq", "exp", None),
            P("seq", "exp", None),
            P("seq", "exp", None),
            P(),
            P(),
            P("exp", None, "seq"),
            P("exp", "seq", None),
            P("seq", None, None),
            P("seq", None, None),
            P("exp"),
            P("exp"),
            P("seq", "exp", None, None, None),
        ),
        out_specs=P("seq", "exp", None),
        check_vma=False,
    )
```

profile of v0, /device:TPU:1, one launch (start us, length us, event | category | flops | bytes accessed | tf_op | source)
XLA Modules:
  0.0 208.6 jit_solution(15001106806405057647)
XLA Ops:
  6.5 2.1 %pad_maximum_fusion = bf16[144,2304]{1,0:T(8,128)(2,1)} fusion(bf16[144,1152]{1,0:T(8,128)(2,1)} %bitcast.114, bf16[144,1152]{1,0:T(8,128)(2,1)} %bitcast.115), kind=kLoop, calls=%fused_computation.33 | loop fusion | flops 1327104 | bytes 1327104 | tf_op jit(solution)/shard_map/concatenate | solution.py:14
  14.2 11.8 %all-to-all-start.1 = ((bf16[64,16,216]{2,0,1:T(8,128)(2,1)}), bf16[64,16,216]{2,0,1:T(8,128)(2,1)S(1)}, u32[]{:S(2)}, u32[]{:S(2)}) async-start(bf16[64,16,216]{2,0,1:T(8,128)(2,1)} %pad_maximum_fusion.1), calls=%async_computation.1 | async-start | bytes 1048576 | tf_op jit(solution)/shard_map/all_to_all | solution.py:37
  28.3 2.0 copy.88
  32.9 14.3 %all-to-all-done.1 = bf16[64,16,216]{2,0,1:T(8,128)(2,1)S(1)} async-done(((bf16[64,16,216]{2,0,1:T(8,128)(2,1)}), bf16[64,16,216]{2,0,1:T(8,128)(2,1)S(1)}, u32[]{:S(2)}, u32[]{:S(2)}) %all-to-all-start.1) | async-done | bytes 442400 | tf_op jit(solution)/shard_map/all_to_all | solution.py:37
  48.0 3.9 %all-to-all-start = ((f32[16,1,4608]{2,1,0:T(1,128)}), f32[16,1,4608]{2,1,0:T(1,128)S(1)}, u32[]{:S(2)}, u32[]{:S(2)}) async-start(f32[16,1,4608]{2,1,0:T(1,128)} %broadcast_in_dim.11), calls=%async_computation | async-start | bytes 589824 | tf_op jit(solution)/shard_map/all_to_all | solution.py:25
  55.6 1.6 reduce.19
  58.6 8.9 %all-to-all-done = f32[16,1,4608]{2,1,0:T(1,128)S(1)} async-done(((f32[16,1,4608]{2,1,0:T(1,128)}), f32[16,1,4608]{2,1,0:T(1,128)S(1)}, u32[]{:S(2)}, u32[]{:S(2)}) %all-to-all-start) | async-done | bytes 294944 | tf_op jit(solution)/shard_map/all_to_all | solution.py:25
  67.4 4.1 %all-to-all-start.2 = ((bf16[16,2,2304]{2,1,0:T(2,128)(2,1)}), bf16[16,2,2304]{2,1,0:T(2,128)(2,1)}, u32[]{:S(2)}, u32[]{:S(2)}) async-start(bf16[16,2,2304]{2,1,0:T(2,128)(2,1)} %reshape.275), calls=%async_computation.2 | async-start | bytes 294912 | tf_op jit(solution)/shard_map/all_to_all | solution.py:125
  71.8 10.9 %all-to-all-done.2 = bf16[16,2,2304]{2,1,0:T(2,128)(2,1)} async-done(((bf16[16,2,2304]{2,1,0:T(2,128)(2,1)}), bf16[16,2,2304]{2,1,0:T(2,128)(2,1)}, u32[]{:S(2)}, u32[]{:S(2)}) %all-to-all-start.2) | async-done | bytes 147488 | tf_op jit(solution)/shard_map/all_to_all | solution.py:125
  82.7 1.8 reshape.276
  85.8 1.6 fusion.62
  88.7 1.9 scatter_custom_fusion
  91.8 42.2 %all_to_all.48 = bf16[32,10,1152]{2,1,0:T(8,128)(2,1)} all-to-all(bf16[32,10,1152]{2,1,0:T(8,128)(2,1)S(1)} %bitcast.106), channel_id=1, replica_groups=mesh['seq'=16,'exp'=32] {'exp'}, dimensions={0} | all-to-all | bytes 1474560 | tf_op jit(solution)/shard_map/all_to_all | solution.py:166
  134.0 2.2 %reshape.242 = bf16[320,1152]{1,0:T(8,128)(2,1)} reshape(bf16[32,10,1152]{2,1,0:T(8,128)(2,1)} %all_to_all.48) | data formatting | bytes 1474560 | tf_op jit(solution)/shard_map/reshape | solution.py:167
  136.1 5.1 %fusion.15 = bf16[320,2304]{1,0:T(8,128)(2,1)S(1)} fusion(bf16[320,1152]{1,0:T(8,128)(2,1)} %reshape.242, bf16[2304,2304]{1,0:T(8,128)(2,1)} %all-gather.2.cloned.1.call-done), kind=kOutput, calls=%fused_computation.18 | convolution fusion | flops 1705328640 | bytes 7520256 | tf_op jit(solution)/shard_map/dot_general | solution.py:168
  141.9 3.0 %fusion.18 = bf16[320,1152]{1,0:T(8,128)(2,1)} fusion(bf16[320,2304]{1,0:T(8,128)(2,1)S(1)} %fusion.15, bf16[2304,2304]{1,0:T(8,128)(2,1)S(1)} %copy-done.5), kind=kOutput, calls=%fused_computation.19 | convolution fusion | flops 1699061760 | bytes 7520256 | tf_op jit(solution)/shard_map/dot_general | solution.py:170
  144.9 2.2 %reshape.243 = bf16[32,10,1152]{2,1,0:T(8,128)(2,1)} reshape(bf16[320,1152]{1,0:T(8,128)(2,1)} %fusion.18) | data formatting | bytes 1474560 | tf_op jit(solution)/shard_map/reshape | solution.py:173
  147.1 2.3 %copy.79 = bf16[32,10,1152]{2,0,1:T(8,128)(2,1)} copy(bf16[32,10,1152]{2,1,0:T(8,128)(2,1)} %reshape.243) | data formatting | bytes 1474560 | tf_op jit(solution)/shard_map/reshape | solution.py:173
  149.4 1.9 collective-permute-start
  151.4 16.9 %collective-permute-done = bf16[32,10,1152]{2,0,1:T(8,128)(2,1)} collective-permute-done((bf16[32,10,1152]{2,0,1:T(8,128)(2,1)}, bf16[32,10,1152]{2,0,1:T(8,128)(2,1)}, u32[]{:S(2)}, u32[]{:S(2)}) %collective-permute-start) | collective-permute-done | bytes 737312 | tf_op jit(solution)/shard_map/ppermute | solution.py:54
  169.5 2.4 %add_convert_fusion = bf16[32,10,576]{2,1,0:T(8,128)(2,1)} fusion(bf16[32,10,576]{2,0,1:T(8,128)(2,1)S(1)} %constant_dynamic-slice_fusion, bf16[32,10,1152]{2,1,0:T(8,128)(2,1)} %reshape.243, s32[]{:T(128)S(6)} %select_n.27), kind=kLoop, calls=%fused_computation.26 | loop fusion | flops 737280 | bytes 1105924 | tf_op jit(solution)/shard_map/convert_element_type | solution.py:175
  171.9 4.6 %all-to-all-start.4 = ((bf16[32,10,576]{2,1,0:T(8,128)(2,1)}), bf16[32,10,576]{2,1,0:T(8,128)(2,1)}, u32[]{:S(2)}, u32[]{:S(2)}) async-start(bf16[32,10,576]{2,1,0:T(8,128)(2,1)} %add_convert_fusion), calls=%async_computation.4 | async-start | bytes 1310720 | tf_op jit(solution)/shard_map/all_to_all | solution.py:181
  176.7 17.5 %all-to-all-done.4 = bf16[32,10,576]{2,1,0:T(8,128)(2,1)} async-done(((bf16[32,10,576]{2,1,0:T(8,128)(2,1)}), bf16[32,10,576]{2,1,0:T(8,128)(2,1)}, u32[]{:S(2)}, u32[]{:S(2)}) %all-to-all-start.4) | async-done | bytes 368672 | tf_op jit(solution)/shard_map/all_to_all | solution.py:181
  194.2 2.2 %copy.104 = bf16[16,2,10,576]{3,1,2,0:T(2,128)(2,1)} copy(bf16[16,2,10,576]{3,2,1,0:T(8,128)(2,1)} %bitcast.29) | data formatting | bytes 737280 | tf_op jit(solution)/shard_map/reshape | solution.py:183
  (68 shorter events, 26.3 us)
Async XLA Ops:
  6.5 79.3 %copy-start = (bf16[1152,1152]{1,0:T(8,128)(2,1)S(1)}, bf16[1152,1152]{1,0:T(8,128)(2,1)}, u32[]{:S(2)}) copy-start(bf16[1152,1152]{1,0:T(8,128)(2,1)} %param.17) | copy-start | bytes 7962628
  6.5 129.6 %all-gather.2.cloned.1.call-start = ((), (), s32[]{:S(2)}) async-start(), calls=%async_computation.5 | async-start | bytes 11280384 | tf_op jit(solution)/shard_map/all_gather | solution.py:15
  10.2 20.1 %copy-start.4 = (s32[1,1,64,1,2]{2,4,3,1,0:T(2,128)S(1)}, s32[1,1,64,1,2]{2,4,3,1,0:T(2,128)}, u32[]{:S(2)}) copy-start(s32[1,1,64,1,2]{2,4,3,1,0:T(2,128)} %param.25) | copy-start | bytes 1540
  14.2 32.9 %all-to-all-start.1 = ((bf16[64,16,216]{2,0,1:T(8,128)(2,1)}), bf16[64,16,216]{2,0,1:T(8,128)(2,1)S(1)}, u32[]{:S(2)}, u32[]{:S(2)}) async-start(bf16[64,16,216]{2,0,1:T(8,128)(2,1)} %pad_maximum_fusion.1), calls=%async_computation.1 | async-start | bytes 1048576 | tf_op jit(solution)/shard_map/all_to_all | solution.py:37
  48.0 19.5 %all-to-all-start = ((f32[16,1,4608]{2,1,0:T(1,128)}), f32[16,1,4608]{2,1,0:T(1,128)S(1)}, u32[]{:S(2)}, u32[]{:S(2)}) async-start(f32[16,1,4608]{2,1,0:T(1,128)} %broadcast_in_dim.11), calls=%async_computation | async-start | bytes 589824 | tf_op jit(solution)/shard_map/all_to_all | solution.py:25
  67.4 15.3 %all-to-all-start.2 = ((bf16[16,2,2304]{2,1,0:T(2,128)(2,1)}), bf16[16,2,2304]{2,1,0:T(2,128)(2,1)}, u32[]{:S(2)}, u32[]{:S(2)}) async-start(bf16[16,2,2304]{2,1,0:T(2,128)(2,1)} %reshape.275), calls=%async_computation.2 | async-start | bytes 294912 | tf_op jit(solution)/shard_map/all_to_all | solution.py:125
  87.8 0.7 copy-start.1
  136.1 5.8 %copy-start.5 = (bf16[2304,2304]{1,0:T(8,128)(2,1)S(1)}, bf16[2304,2304]{1,0:T(8,128)(2,1)}, u32[]{:S(2)}) copy-start(bf16[2304,2304]{1,0:T(8,128)(2,1)} %all-gather.2.cloned.1.call-done) | copy-start | bytes 31850500
  147.1 29.4 %copy-start.2 = (bf16[64,1152]{1,0:T(8,128)(2,1)S(1)}, bf16[64,1152]{1,0:T(8,128)(2,1)}, u32[]{:S(2)}) copy-start(bf16[64,1152]{1,0:T(8,128)(2,1)} %copy-done.1) | copy-start | bytes 442372
  147.1 29.4 %copy-start.3 = (bf16[1152,16]{0,1:T(8,128)(2,1)S(1)}, bf16[1152,16]{0,1:T(8,128)(2,1)}, u32[]{:S(2)}) copy-start(bf16[1152,16]{0,1:T(8,128)(2,1)} %param.18) | copy-start | bytes 110596
  149.4 18.9 %collective-permute-start = (bf16[32,10,1152]{2,0,1:T(8,128)(2,1)}, bf16[32,10,1152]{2,0,1:T(8,128)(2,1)}, u32[]{:S(2)}, u32[]{:S(2)}) collective-permute-start(bf16[32,10,1152]{2,0,1:T(8,128)(2,1)} %copy.79), channel_id=1, source_target_pairs={{0,1},{1,0},{2,3},{3,2},{4,5},{5,4},{6,7},{7,6},{8,9},{9,8},{10,11... | collective-permute-start | bytes 2211848 | tf_op jit(solution)/shard_map/ppermute | solution.py:54
  171.9 22.3 %all-to-all-start.4 = ((bf16[32,10,576]{2,1,0:T(8,128)(2,1)}), bf16[32,10,576]{2,1,0:T(8,128)(2,1)}, u32[]{:S(2)}, u32[]{:S(2)}) async-start(bf16[32,10,576]{2,1,0:T(8,128)(2,1)} %add_convert_fusion), calls=%async_computation.4 | async-start | bytes 1310720 | tf_op jit(solution)/shard_map/all_to_all | solution.py:181
Sparse Core Ops, SparseCore 0:
  9.5 92.8 all-gather.1
where the time goes:
time: 211 us; the launch traced here: 209 us
  waiting for transfers between devices  68.4 us (32%)
  blocking collectives  42.2 us (20%)
  local copies, waits for them, and re-layouts  33 us (16%)
  starting transfers between devices  26.3 us (12%)
  between operations  15 us (7%)
  matrix products  13.7 us (6%)
  other arithmetic  9.93 us (5%)
    all_to_all x1, blocking collectives, body(): lax.all_to_all(outgoing, 'exp', split_axis=0, concat_axis=0, tiled=True)  42.2 us
    all_to_all x1, waiting for transfers between devices, body(): lax.all_to_all(produced_half, 'exp', split_axis=0, concat_axis=0, tiled=T...  17.5 us
    ppermute x1, waiting for transfers between devices, swapped(): return lax.ppermute(block, axis, route)  16.9 us
    all_to_all x1, waiting for transfers between devices, side_by_side(): lax.all_to_all(both, axis, split_axis=split_dim, concat_axis=concat_dim,...  14.3 us
    all_to_all x1, starting transfers between devices, side_by_side(): lax.all_to_all(both, axis, split_axis=split_dim, concat_axis=concat_dim,...  11.8 us
    all_to_all x1, waiting for transfers between devices, body(): lax.all_to_all(mixed_out, 'seq', split_axis=0, concat_axis=1, tiled=True)  10.9 us
    all_to_all x1, waiting for transfers between devices, from_everyone(): lax.all_to_all(jnp.broadcast_to(value[None], (peers, *value.shape)), axis...  8.87 us
    unnamed x18, local copies, waits for them, and re-layouts  7.59 us
  transfers between devices with their start and end apart: 6, of which 5 were waited for; matrix products, arithmetic and copies ran while one was open for 14% of the time, Pallas kernels for 0%

commit v1 on v0

v1 whole, which is shorter than its diff:
```python
import functools
import math

import jax
import jax.numpy as jnp
from jax import lax
from jax.experimental import pallas as pl
from jax.experimental.pallas import tpu as pltpu
from jax.sharding import PartitionSpec as P

HEAD = 72
FREQ = 256
MESH = pl.DeviceIdType.MESH
NS = 16
NE = 32
NZ = 8
D = 1152
HID = 144
CAP = 10
PAD = 16
TILES = 9
NT = (((1,), (1,)), ((), ()))
NN = (((1,), (0,)), ((), ()))
F32 = jnp.float32
BF = jnp.bfloat16


def mm(a, b, dims=NN):
    return lax.dot_general(a, b, dims, preferred_element_type=F32)


def rcopy(src, dst, ssem, rsem, axis, peer):
    return pltpu.make_async_remote_copy(
        src_ref=src, dst_ref=dst, send_sem=ssem, recv_sem=rsem,
        device_id={axis: peer}, device_id_type=MESH,
    )


def kernel(
    q_ref, k_ref, v_ref, res_ref, ids_ref, label_ref, emb_ref, tw_ref, rt_ref,
    ct_hbm, wo_hbm, w1_hbm, w2_hbm, out_ref,
    qsend, qrecv, kk, vv, osend, orecv, att, ct, wo, cpart, crecv, cond,
    wbuf, moe_s, upd_s, wt, xsend, xrecv, acc, ysend, yrecv,
    q_ss, q_rs, o_ss, o_rs, c1_ss, c1_rs, c2_ss, c2_rs,
    cw_ss, ccw_ss, dd_ss, w_rs, x_ss, x_rs, y_ss, y_rs, l_s,
):
    s = lax.axis_index("seq")
    e = lax.axis_index("exp")
    z, c = s // 2, s % 2

    lw1 = pltpu.make_async_copy(w1_hbm, wbuf.at[s, 0], l_s.at[0])
    lw2 = pltpu.make_async_copy(w2_hbm, wbuf.at[s, 1], l_s.at[1])
    lct = pltpu.make_async_copy(ct_hbm, ct, l_s.at[2])
    lwo = pltpu.make_async_copy(wo_hbm, wo, l_s.at[3])
    lct.start()
    lw1.start()
    lw2.start()
    lwo.start()

    barrier = pltpu.get_barrier_semaphore()

    @pl.loop(1, NS)
    def _(d):
        pl.semaphore_signal(barrier, inc=1, device_id={"seq": (s + d) % NS}, device_id_type=MESH)

    @pl.loop(1, NE)
    def _(d):
        pl.semaphore_signal(barrier, inc=1, device_id={"exp": (e + d) % NE}, device_id_type=MESH)

    for h in range(NS):
        lanes = slice(h * HEAD, (h + 1) * HEAD)
        qsend[h, :, 0:HEAD] = q_ref[:, lanes]
        qsend[h, :, HEAD : 2 * HEAD] = k_ref[:, lanes]
        qsend[h, :, 2 * HEAD : 3 * HEAD] = v_ref[:, lanes]

    pl.semaphore_wait(barrier, NS - 1 + NE - 1)

    def qcopy(to, frm):
        return rcopy(qsend.at[to], qrecv.at[frm], q_ss.at[to], q_rs.at[frm], "seq", to)

    @pl.loop(1, NS)
    def _(d):
        qcopy((s + d) % NS, s).start()

    qrecv[s] = qsend[s]

    lct.wait()
    place = label_ref[0] - s * 64
    row = ct[jnp.clip(place, 0, 63)].astype(F32)
    part = jnp.where((place >= 0) & (place < 64), row, 0.0)
    for r in range(FREQ // NS):
        part = part + emb_ref[r] * tw_ref[r].astype(F32)
    for t in range(TILES):
        cpart[t] = part[:, t * 128 : (t + 1) * 128]

    def c1copy(to, frm):
        return rcopy(cpart.at[to], crecv.at[frm], c1_ss.at[to], c1_rs.at[frm], "seq", to)

    for t in range(TILES):
        @pl.when(s != t)
        def _(t=t):
            c1copy(t, s).start()

    @pl.when(s < TILES)
    def _():
        crecv[s] = cpart[s]

    @pl.loop(1, NS)
    def _(d):
        qcopy(s, (s + d) % NS).wait_recv()

    full = qrecv[...].reshape(NS * 64, 256)
    kk[...] = full[:, HEAD : 2 * HEAD]
    vv[...] = full[:, 2 * HEAD : 3 * HEAD]
    scale = 1.0 / math.sqrt(HEAD)

    def ocopy(to, frm):
        return rcopy(osend.at[to], orecv.at[frm], o_ss.at[to], o_rs.at[frm], "seq", to)

    @pl.loop(0, 4)
    def _(b):
        query = qrecv[pl.ds(b * 4, 4)].reshape(256, 256)[:, 0:HEAD]
        scores = mm(query, kk[...], NT) * scale
        top = jnp.max(scores, axis=-1, keepdims=True)
        w = jnp.exp(scores - top)
        total = jnp.sum(w, axis=-1, keepdims=True)
        o = mm(w.astype(BF), vv[...]) / total
        osend[pl.ds(b * 4, 4), :, 0:HEAD] = o.astype(BF).reshape(4, 64, HEAD)

        @pl.loop(0, 4)
        def _(i):
            j = b * 4 + i

            @pl.when(j != s)
            def _():
                ocopy(j, s).start()

    orecv[s] = osend[s]

    def ring(k, way, p):
        owner = (z + NZ - k) % NZ if way == 0 else (z + k) % NZ
        slot = owner * 2 + c
        to = ((z + 1) % NZ if way == 0 else (z + NZ - 1) % NZ) * 2 + c
        sems = cw_ss if way == 0 else ccw_ss
        return rcopy(wbuf.at[slot, p], wbuf.at[slot, p], sems.at[k, p], w_rs.at[slot, p], "seq", to)

    def arrival(k, way, p):
        owner = (z + 2 * NZ - 1 - k) % NZ if way == 0 else (z + 1 + k) % NZ
        slot = owner * 2 + c
        return rcopy(wbuf.at[slot, p], wbuf.at[slot, p], cw_ss.at[0, p], w_rs.at[slot, p], "seq", z * 2 + 1 - c)

    def across(owner, p, mine):
        slot = owner * 2 + (c if mine else 1 - c)
        return rcopy(wbuf.at[slot, p], wbuf.at[slot, p], dd_ss.at[owner, p], w_rs.at[slot, p], "seq", z * 2 + 1 - c)

    lw1.wait()
    lw2.wait()
    for p in range(2):
        ring(0, 0, p).start()
        ring(0, 1, p).start()
    for p in range(2):
        across(z, p, True).start()

    @pl.loop(0, NS)
    def _(i):
        @pl.when((s < TILES) & (i != s))
        def _():
            rcopy(cpart.at[0], crecv.at[i], c1_ss.at[0], c1_rs.at[i], "seq", (s + 1) % NS).wait_recv()

    def c2copy(tile, to):
        return rcopy(cond.at[tile], cond.at[tile], c2_ss.at[to], c2_rs.at[tile], "seq", to)

    @pl.when(s < TILES)
    def _():
        cond[s] = jnp.sum(crecv[...], axis=0)

        @pl.loop(1, NS)
        def _(d):
            c2copy(s, (s + d) % NS).start()

    ids0 = ids_ref[0:1, :]
    ids1 = ids_ref[1:2, :]
    rows = lax.broadcasted_iota(jnp.int32, (16 * PAD, 64), 0)
    of_e, of_s = rows // PAD, (rows % PAD).astype(F32)
    hit0, hit1 = ids0 == of_e, ids1 == of_e
    named = jnp.where(hit0 | hit1, 1.0, 0.0)
    earlier = jnp.where(
        lax.broadcasted_iota(jnp.int32, (64, 64), 0) < lax.broadcasted_iota(jnp.int32, (64, 64), 1), 1.0, 0.0
    )
    slot = mm(named.astype(BF), earlier.astype(BF))
    here = slot == of_s
    pick0 = jnp.where(hit0 & here, 1.0, 0.0)
    pick1 = jnp.where(hit1 & here, 1.0, 0.0)

    @pl.loop(1, NS)
    def _(d):
        ocopy(s, (s + d) % NS).wait_recv()

    for h in range(NS):
        att[:, h * HEAD : (h + 1) * HEAD] = orecv[h, :, 0:HEAD]
    lwo.wait()
    projected = mm(att[...], wo[...])

    for t in range(TILES):
        @pl.when(s != t)
        def _(t=t):
            c2copy(t, (s + 1) % NS).wait_recv()

    mods = jnp.concatenate([cond[t] for t in range(TILES)], axis=1)
    updated = (res_ref[...].astype(F32) + mods[0:1, :] * projected).astype(BF)
    upd_s[...] = updated
    updated_f = updated.astype(F32)
    mean = jnp.mean(updated_f, axis=-1, keepdims=True)
    centered = updated_f - mean
    variance = jnp.mean(centered * centered, axis=-1, keepdims=True)
    moe_in = (centered * lax.rsqrt(variance + 1e-6) * (1.0 + mods[2:3, :]) + mods[1:2, :]).astype(BF)

    xsend[...] = mm((pick0 + pick1).astype(BF), moe_in).astype(BF).reshape(16, PAD, D)

    def xcopy(to, frm):
        return rcopy(
            xsend.at[to // 2, pl.ds(0, ROWS)], xrecv.at[frm, pl.ds(0, ROWS)], x_ss.at[to], x_rs.at[frm], "exp", to
        )

    @pl.loop(1, NE)
    def _(d):
        xcopy((e + d) % NE, e).start()

    xrecv[e] = xsend[e // 2]

    logits = mm(rt_ref[...], moe_in, NT)
    experts = lax.broadcasted_iota(jnp.int32, (16, 64), 0)
    chosen0 = jnp.sum(jnp.where(experts == ids0, logits, 0.0), axis=0, keepdims=True)
    chosen1 = jnp.sum(jnp.where(experts == ids1, logits, 0.0), axis=0, keepdims=True)
    share = 1.0 / (1.0 + jnp.exp(-(chosen0 - chosen1)))
    weight = pick0 * share + pick1 * (1.0 - share)
    high = weight.astype(BF)
    low = (weight - high.astype(F32)).astype(BF)
    eye = jnp.where(
        lax.broadcasted_iota(jnp.int32, (64, 64), 0) == lax.broadcasted_iota(jnp.int32, (64, 64), 1), 1.0, 0.0
    ).astype(BF)
    wt[0] = mm(eye, high, NT).astype(BF)
    wt[1] = mm(eye, low, NT).astype(BF)

    def step(k, last):
        for p in range(2):
            for way in range(2):
                owner = (z + 2 * NZ - 1 - k) % NZ if way == 0 else (z + 1 + k) % NZ
                arrival(k, way, p).wait_recv()
                if last:
                    if way == p:
                        ring(k + 1, way, p).start()
                else:
                    ring(k + 1, way, p).start()
                across(owner, p, True).start()

    step(0, False)

    @pl.loop(1, NE)
    def _(d):
        xcopy(e, (e + d) % NE).wait_recv()

    def ffn(owner, first):
        across(owner, 0, False).wait_recv()
        across(owner, 1, False).wait_recv()
        w1 = wbuf[pl.ds(owner * 2, 2), 0].reshape(2 * HID, D)
        w2 = wbuf[pl.ds(owner * 2, 2), 1].reshape(2 * HID, D)
        for b in range(NB):
            x = xrecv[b * (NE // NB) : (b + 1) * (NE // NB)].reshape(NE // NB * PAD, D)
            hidden = jax.nn.gelu(mm(x, w1, NT), approximate=True).astype(BF)
            y = mm(hidden, w2)
            if first:
                acc[b] = y
            else:
                acc[b] = acc[b] + y

    ffn(z, True)

    @pl.loop(0, 3)
    def _(k):
        @pl.when(k > 0)
        def _():
            for p in range(2):
                for way in range(2):
                    owner = (z + 2 * NZ - 1 - k) % NZ if way == 0 else (z + 1 + k) % NZ
                    arrival(k, way, p).wait_recv()
                    if way == p:
                        ring(k + 1, way, p).start()
                    else:
                        @pl.when(k < 2)
                        def _():
                            ring(k + 1, way, p).start()
                    across(owner, p, True).start()

        @pl.loop(0, 2)
        def _(way):
            ffn(jnp.where(way == 0, (z + 2 * NZ - 1 - k) % NZ, (z + 1 + k) % NZ), False)

    far = (z + 4) % NZ
    arrival(3, 0, 0).wait_recv()
    across(far, 0, True).start()
    arrival(3, 1, 1).wait_recv()
    across(far, 1, True).start()
    across(far, 0, False).wait_recv()
    across(far, 1, False).wait_recv()
    w1 = wbuf[pl.ds(far * 2, 2), 0].reshape(2 * HID, D)
    w2 = wbuf[pl.ds(far * 2, 2), 1].reshape(2 * HID, D)

    def ycopy(to, frm):
        return rcopy(ysend.at[to, pl.ds(0, ROWS)], yrecv.at[frm, pl.ds(0, ROWS)], y_ss.at[to], y_rs.at[frm], "exp", to)

    @pl.loop(0, NB)
    def _(b):
        first = b * (NE // NB)
        x = xrecv[pl.ds(first, NE // NB)].reshape(NE // NB * PAD, D)
        hidden = jax.nn.gelu(mm(x, w1, NT), approximate=True).astype(BF)
        y = acc[b] + mm(hidden, w2)
        ysend[pl.ds(first, NE // NB)] = y.astype(BF).reshape(NE // NB, PAD, D)

        @pl.loop(0, NE // NB)
        def _(i):
            @pl.when(first + i != e)
            def _():
                ycopy(first + i, e).start()

    yrecv[e] = ysend[e]

    @pl.loop(1, NE)
    def _(d):
        ycopy(e, (e + d) % NE).wait_recv()

    halves = yrecv[...].reshape(16, 2, PAD, D)
    got = (halves[:, 0].astype(F32) + halves[:, 1].astype(F32)).reshape(16 * PAD, D)
    real = lax.broadcasted_iota(jnp.int32, (16 * PAD, 1), 0) % PAD < CAP
    got = jnp.where(real, got, 0.0).astype(BF)
    mixed = mm(wt[0], got) + mm(wt[1], got)
    gate = jnp.concatenate([cond[t] for t in range(TILES)], axis=1)[3:4, :]
    out_ref[...] = (upd_s[...].astype(F32) + gate * mixed).astype(BF)

    @pl.loop(1, NS)
    def _(d):
        qcopy((s + d) % NS, s).wait_send()
        ocopy((s + d) % NS, s).wait_send()

    for t in range(TILES):
        @pl.when(s != t)
        def _(t=t):
            c1copy(t, s).wait_send()

    @pl.when(s < TILES)
    def _():
        @pl.loop(1, NS)
        def _(d):
            c2copy(s, (s + d) % NS).wait_send()

    for k in range(4):
        for p in range(2):
            for way in range(2):
                if k < 3 or way == p:
                    ring(k, way, p).wait_send()

    @pl.loop(0, NZ)
    def _(i):
        across(i, 0, True).wait_send()
        across(i, 1, True).wait_send()

    @pl.loop(1, NE)
    def _(d):
        xcopy((e + d) % NE, e).wait_send()
        ycopy((e + d) % NE, e).wait_send()


ROWS = PAD
NB = 4


def body(
    residual_in, query_proj, key_proj, value_proj, out_weight, router_weight, first_weight, second_weight,
    class_table, time_weight, class_labels, timesteps, expert_ids,
):
    half = FREQ // 2
    index = lax.axis_index("seq") * (FREQ // NS) + jnp.arange(FREQ // NS, dtype=jnp.int32)
    frequency = jnp.exp(-math.log(10000.0) * (index % half).astype(F32) / half)
    angle = timesteps.astype(F32) * frequency
    emb = jnp.where(index < half, jnp.cos(angle), jnp.sin(angle))
    flat = lambda a: a.reshape(64, D)
    vmem = pl.BlockSpec(memory_space=pltpu.VMEM)
    smem = pl.BlockSpec(memory_space=pltpu.SMEM)
    anyspace = pl.BlockSpec(memory_space=pl.ANY)
    dma = pltpu.SemaphoreType.DMA
    out = pl.pallas_call(
        kernel,
        out_shape=jax.ShapeDtypeStruct((64, D), BF),
        in_specs=[vmem] * 5 + [smem] * 2 + [vmem] * 2 + [anyspace] * 4,
        out_specs=vmem,
        scratch_shapes=[
            pltpu.VMEM((NS, 64, 256), BF),
            pltpu.VMEM((NS, 64, 256), BF),
            pltpu.VMEM((NS * 64, HEAD), BF),
            pltpu.VMEM((NS * 64, HEAD), BF),
            pltpu.VMEM((NS, 64, 128), BF),
            pltpu.VMEM((NS, 64, 128), BF),
            pltpu.VMEM((64, D), BF),
            pltpu.VMEM((64, 4, D), BF),
            pltpu.VMEM((D, D), BF),
            pltpu.VMEM((TILES, 4, 128), F32),
            pltpu.VMEM((NS, 4, 128), F32),
            pltpu.VMEM((TILES, 4, 128), F32),
            pltpu.VMEM((NS, 2, HID, D), BF),
            pltpu.VMEM((64, D), BF),
            pltpu.VMEM((64, D), BF),
            pltpu.VMEM((2, 64, 16 * PAD), BF),
            pltpu.VMEM((16, PAD, D), BF),
            pltpu.VMEM((NE, PAD, D), BF),
            pltpu.VMEM((NB, NE // NB * PAD, D), F32),
            pltpu.VMEM((NE, PAD, D), BF),
            pltpu.VMEM((NE, PAD, D), BF),
            dma((NS,)), dma((NS,)), dma((NS,)), dma((NS,)),
            dma((TILES,)), dma((NS,)), dma((NS,)), dma((TILES,)),
            dma((4, 2)), dma((4, 2)), dma((NZ, 2)), dma((NS, 2)),
            dma((NE,)), dma((NE,)), dma((NE,)), dma((NE,)),
            dma((4,)),
        ],
        compiler_params=pltpu.CompilerParams(
            collective_id=0, has_side_effects=True, vmem_limit_bytes=58 * 1024 * 1024
        ),
    )(
        flat(query_proj), flat(key_proj), flat(value_proj), flat(residual_in),
        expert_ids.reshape(64, 2).T, class_labels, emb, time_weight, router_weight.T,
        class_table, out_weight, jnp.transpose(first_weight[0]), second_weight[0],
    )
    return out.reshape(64, 1, D)


def solution(mesh):
    return jax.shard_map(
        body,
        mesh=mesh,
        in_specs=(
            P("seq", "exp", None),
            P("seq", "exp", None),
            P("seq", "exp", None),
            P("seq", "exp", None),
            P(),
            P(),
            P("exp", None, "seq"),
            P("exp", "seq", None),
            P("seq", None, None),
            P("seq", None, None),
            P("exp"),
            P("exp"),
            P("seq", "exp", None, None, None),
        ),
        out_specs=P("seq", "exp", None),
        check_vma=False,
    )
```

time: 211 us -> 157 us (0.74)
  the two profiles are of different devices: /device:TPU:1 before, /device:TPU:58 now
where the time goes in v1:
time: 157 us
  Pallas kernels  154 us (98%)
  local copies, waits for them, and re-layouts  1.58 us (1%)
    pallas_call x1, Pallas kernels, body(): pl.pallas_call(kernel, out_shape=jax.ShapeDtypeStruct((64, D), BF), in_sp...  154 us

profile of v1, /device:TPU:58, one launch (start us, length us, event | category | flops | bytes accessed | tf_op | source)
XLA Modules:
  0.0 157.2 jit_solution(18205910452652461195)
XLA Ops:
  1.3 0.6 compare_select_fusion.2.emb_ref
  1.9 153.7 %shard_map.127 = bf16[64,1152]{1,0:T(8,128)(2,1)} custom-call(bf16[64,1152]{1,0:T(8,128)(2,1)} %bitcast.17, bf16[64,1152]{1,0:T(8,128)(2,1)} %bitcast.18, bf16[64,1152]{1,0:T(8,128)(2,1)} %bitcast.19, bf16[64,1152]{1,0:T(8,128)(2,1)} %bitcast.20, s32[2,64]{1,0:T(2,128)} %bitcast.22, s32[1]{0:T(128)S(6)} %copy.15.label_ref, f32[16]{0:T(128)} %compare_select_fusion.2.emb_ref, ...), custom_call_target="tpu_custom_call" | custom-call | tf_op jit(solution)/shard_map/pallas_call | solution.py:391
  155.6 1.6 %copy.17 = bf16[64,1,1152]{2,0,1:T(8,128)(2,1)} copy(bf16[64,1,1152]{2,0,1:T(8,128)(2,1)} %bitcast.14) | data formatting | bytes 294912
